TPU v7x, 128 devices: a whole 4x4x4 slice. The times are simulated.
128 devices in a mesh: row: 2 (over core), col: 64 (over z, y, x).
Axes of the slice: x: 4, y: 4, z: 4, core: 2. Of those that a mesh axis runs over, the one named last changes fastest.
Arguments:
- v_panels: float32 [6144, 6144], P('row', 'col')
- t_factors: float32 [192, 32, 32], P('col')
- z_vecs: float32 [6144, 4096], P(None, ('row', 'col'))
Outputs:
- output: float32 [6144, 4096], P(None, ('row', 'col'))
All inputs are finite; a program needn't handle non-finite values.
Results may differ from a plain program's by a relative error of at most 0.001.
Values sent between devices are 32-bit elements.
A program may use at most 1 GiB of HBM per device.

v0:
```python
import jax
import jax.numpy as jnp
from jax import lax
from jax.sharding import PartitionSpec as P, NamedSharding

FULL_PREC = lax.Precision.HIGHEST
CONTRACT_ROWS = (((0,), (0,)), ((), ()))


def solution(mesh):
    col_dev = mesh.shape["col"]

    def local_apply(v_loc, t_loc, z_loc):
        num_local = t_loc.shape[0]
        block_w = t_loc.shape[1]
        x_two = lax.all_to_all(z_loc, "row", 0, 1, tiled=True)

        def outer_step(step_idx, x_cur):
            local_idx = num_local - 1 - step_idx
            v_own = lax.dynamic_slice_in_dim(v_loc, local_idx * block_w, block_w, axis=1)
            t_own = lax.dynamic_index_in_dim(t_loc, local_idx, axis=0, keepdims=False)
            v_all = lax.all_gather(v_own, "col")
            t_all = lax.all_gather(t_own, "col")

            def inner_step(sub_idx, x_in):
                owner_col = col_dev - 1 - sub_idx
                v_blk = v_all[owner_col]
                t_blk = t_all[owner_col]
                w_part = lax.dot_general(v_blk, x_in, CONTRACT_ROWS, precision=FULL_PREC, preferred_element_type=jnp.float32)
                w_sum = lax.psum(w_part, "row")
                y_blk = jnp.dot(t_blk, w_sum, precision=FULL_PREC, preferred_element_type=jnp.float32)
                return x_in - jnp.dot(v_blk, y_blk, precision=FULL_PREC, preferred_element_type=jnp.float32)

            return lax.fori_loop(0, col_dev, inner_step, x_cur)

        x_two = lax.fori_loop(0, num_local, outer_step, x_two)
        return lax.all_to_all(x_two, "row", 1, 0, tiled=True)

    return jax.shard_map(
        local_apply,
        mesh=mesh,
        in_specs=(P("row", "col"), P("col", None, None), P(None, ("row", "col"))),
        out_specs=P(None, ("row", "col")),
        check_vma=False,
    )
```

profile of v0, /device:TPU:1, one launch (start us, length us, event | category | flops | bytes accessed | tf_op | source)
XLA Modules:
  0.0 3369.2 jit_solution(910303851159873770)
XLA Ops:
  8.6 4.9 all-to-all-start
  14.8 3342.6 %while.44 = (s32[]{:T(128)}, f32[3072,64]{0,1:T(8,128)S(1)}, f32[3072,96]{0,1:T(8,128)}, f32[3,32,32]{2,1,0:T(8,128)}, s32[]{:T(128)}, /*index=5*/s32[]{:T(128)}...) while((s32[]{:T(128)}, f32[3072,64]{0,1:T(8,128)S(1)}, ...), condition=%wide.region_4.5_spmd, body=%wide.region_0.4_spmd.sunk | while | flops 151980048 | bytes 160780800 | solution.py:36
  18.2 165.4 %all_gather.32 = f32[64,32,32]{2,1,0:T(8,128)S(1)} all-gather(f32[1,32,32]{2,1,0:T(8,128)S(1)} %constant_dynamic-slice_fusion.5), channel_id=1, replica_groups=mesh['row'=2,'col'=64] {'col'}, dimensions={0}, use_global_device_ids=true | all-gather | bytes 266240 | tf_op jit(solution)/shard_map/while/body/eval_jaxpr/all_gather | solution.py:23
  183.6 239.7 %all-gather.5.cloned.1.call-done = f32[196608,32]{1,0:T(8,128)} async-done(((f32[3072,32]{1,0:T(8,128)}), f32[196608,32]{1,0:T(8,128)}) %all-gather.5.cloned.1.call-update) | async-done | bytes 25165840 | tf_op jit(solution)/shard_map/while/body/eval_jaxpr/all_gather | solution.py:22
  423.3 708.7 %while.45 = (s32[]{:T(128)}, f32[3072,64]{0,1:T(8,128)S(1)}, f32[64,3072,32]{2,1,0:T(8,128)}, f32[64,32,32]{2,1,0:T(8,128)S(1)}, s32[]{:T(128)}, /*index=5*/s32[]{:T(128)}, s32[]{:T(128)}, s32[]{:T(128)}) while((s32[]{:T(128)}, f32[3072,64]{0,1:T(8,128)S(1)}, f32[64,3072,32]{2,1,0:T(8,128)}, f32[64,32,32]{2,1,0:T(8,128)S(1)}, s32[]{:T(128)}, ...), condition=%wide.region_3.3_spmd, body=%wide.region_1.2_spmd.sunk | while | flops 151980032 | bytes 5578895 | solution.py:34
  427.3 4.1 psum.14
  457.2 4.0 fusion.28
  468.2 4.0 fusion.28
  490.3 4.0 fusion.28
  523.6 4.0 fusion.28
  534.6 4.0 fusion.28
  545.7 4.0 fusion.28
  556.7 4.0 fusion.28
  590.0 4.0 fusion.28
  601.0 4.0 fusion.28
  612.1 4.0 fusion.28
  623.1 4.0 fusion.28
  656.4 4.0 fusion.28
  678.5 4.0 fusion.28
  689.5 4.0 fusion.28
  722.8 4.0 fusion.28
  744.9 4.0 fusion.28
  755.9 4.0 fusion.28
  811.3 4.0 fusion.28
  822.3 4.0 fusion.28
  844.4 4.0 fusion.28
  877.7 4.0 fusion.28
  888.7 4.0 fusion.28
  910.8 4.0 fusion.28
  944.1 4.0 fusion.28
  955.1 4.0 fusion.28
  966.2 4.0 fusion.28
  977.2 4.0 fusion.28
  1010.5 4.0 fusion.28
  1021.4 4.0 fusion.28
  1032.6 4.0 fusion.28
  1043.6 4.0 fusion.28
  1076.9 4.0 fusion.28
  1099.0 4.0 fusion.28
  1110.0 4.0 fusion.28
  1135.6 160.9 %all_gather.32 = f32[64,32,32]{2,1,0:T(8,128)S(1)} all-gather(f32[1,32,32]{2,1,0:T(8,128)S(1)} %constant_dynamic-slice_fusion.5), channel_id=1, replica_groups=mesh['row'=2,'col'=64] {'col'}, dimensions={0}, use_global_device_ids=true | all-gather | bytes 266240 | tf_op jit(solution)/shard_map/while/body/eval_jaxpr/all_gather | solution.py:23
  1296.4 239.6 %all-gather.5.cloned.1.call-done = f32[196608,32]{1,0:T(8,128)} async-done(((f32[3072,32]{1,0:T(8,128)}), f32[196608,32]{1,0:T(8,128)}) %all-gather.5.cloned.1.call-update) | async-done | bytes 25165840 | tf_op jit(solution)/shard_map/while/body/eval_jaxpr/all_gather | solution.py:22
  1536.0 708.7 %while.45 = (s32[]{:T(128)}, f32[3072,64]{0,1:T(8,128)S(1)}, f32[64,3072,32]{2,1,0:T(8,128)}, f32[64,32,32]{2,1,0:T(8,128)S(1)}, s32[]{:T(128)}, /*index=5*/s32[]{:T(128)}, s32[]{:T(128)}, s32[]{:T(128)}) while((s32[]{:T(128)}, f32[3072,64]{0,1:T(8,128)S(1)}, f32[64,3072,32]{2,1,0:T(8,128)}, f32[64,32,32]{2,1,0:T(8,128)S(1)}, s32[]{:T(128)}, ...), condition=%wide.region_3.3_spmd, body=%wide.region_1.2_spmd.sunk | while | flops 151980032 | bytes 5578895 | solution.py:34
  1540.0 4.1 psum.14
  1547.7 4.0 fusion.28
  1569.9 4.0 fusion.28
  1580.9 4.0 fusion.28
  1603.0 4.0 fusion.28
  1614.1 4.0 fusion.28
  1636.3 4.0 fusion.28
  1647.3 4.0 fusion.28
  1669.4 4.0 fusion.28
  1680.5 4.0 fusion.28
  1702.7 4.0 fusion.28
  1735.8 4.0 fusion.28
  1769.1 4.0 fusion.28
  1802.2 4.0 fusion.28
  1835.4 4.0 fusion.28
  1868.6 4.0 fusion.28
  2248.2 160.8 %all_gather.32 = f32[64,32,32]{2,1,0:T(8,128)S(1)} all-gather(f32[1,32,32]{2,1,0:T(8,128)S(1)} %constant_dynamic-slice_fusion.5), channel_id=1, replica_groups=mesh['row'=2,'col'=64] {'col'}, dimensions={0}, use_global_device_ids=true | all-gather | bytes 266240 | tf_op jit(solution)/shard_map/while/body/eval_jaxpr/all_gather | solution.py:23
  2409.1 239.6 %all-gather.5.cloned.1.call-done = f32[196608,32]{1,0:T(8,128)} async-done(((f32[3072,32]{1,0:T(8,128)}), f32[196608,32]{1,0:T(8,128)}) %all-gather.5.cloned.1.call-update) | async-done | bytes 25165840 | tf_op jit(solution)/shard_map/while/body/eval_jaxpr/all_gather | solution.py:22
  2648.7 708.7 %while.45 = (s32[]{:T(128)}, f32[3072,64]{0,1:T(8,128)S(1)}, f32[64,3072,32]{2,1,0:T(8,128)}, f32[64,32,32]{2,1,0:T(8,128)S(1)}, s32[]{:T(128)}, /*index=5*/s32[]{:T(128)}, s32[]{:T(128)}, s32[]{:T(128)}) while((s32[]{:T(128)}, f32[3072,64]{0,1:T(8,128)S(1)}, f32[64,3072,32]{2,1,0:T(8,128)}, f32[64,32,32]{2,1,0:T(8,128)S(1)}, s32[]{:T(128)}, ...), condition=%wide.region_3.3_spmd, body=%wide.region_1.2_spmd.sunk | while | flops 151980032 | bytes 5578895 | solution.py:34
  2652.7 4.1 psum.14
  3357.4 4.3 all_to_all.38
  (734 shorter events, 1927.4 us)
Async XLA Ops:
  8.6 6.2 all-to-all-start
  14.8 408.5 %all-gather.5.cloned.1.call-start = ((), (), s32[]{:S(2)}) async-start(), calls=%async_computation.2 | async-start | bytes 102236160 | tf_op jit(solution)/shard_map/while/body/eval_jaxpr/all_gather | solution.py:22
  1132.1 403.9 %all-gather.5.cloned.1.call-start = ((), (), s32[]{:S(2)}) async-start(), calls=%async_computation.2 | async-start | bytes 102236160 | tf_op jit(solution)/shard_map/while/body/eval_jaxpr/all_gather | solution.py:22
  2244.8 403.9 %all-gather.5.cloned.1.call-start = ((), (), s32[]{:S(2)}) async-start(), calls=%async_computation.2 | async-start | bytes 102236160 | tf_op jit(solution)/shard_map/while/body/eval_jaxpr/all_gather | solution.py:22
Sparse Core Ops, SparseCore 0:
  18.4 404.9 all-gather.4
  1135.7 400.3 all-gather.4
  2248.3 400.2 all-gather.4
where the time goes:
time: 3380 us; the launch traced here: 3370 us
  matrix products  1460 us (43%)
  blocking collectives  1150 us (34%)
  waiting for transfers between devices  720 us (21%)
    dot_general x192, matrix products, inner_step(): lax.dot_general(v_blk, x_in, CONTRACT_ROWS, precision=FULL_PREC, preferre...  765 us
    all_gather x3, waiting for transfers between devices, outer_step(): v_all = lax.all_gather(v_own, 'col')  719 us
    dot_general x192, matrix products, inner_step(): jnp.dot(v_blk, y_blk, precision=FULL_PREC, preferred_element_type=jnp.flo...  666 us
    psum x192, blocking collectives, inner_step(): w_sum = lax.psum(w_part, 'row')  664 us
    all_gather x3, blocking collectives, outer_step(): t_all = lax.all_gather(t_own, 'col')  487 us
  transfers between devices with their start and end apart: 4, of which 4 were waited for; matrix products, arithmetic and copies ran while one was open for 0% of the time, Pallas kernels for 0%

commit v1 on v0

v1 whole, which is shorter than its diff:
```python
import functools

import jax
import jax.numpy as jnp
from jax import lax
from jax.experimental import pallas as pl
from jax.experimental.pallas import tpu as pltpu
from jax.sharding import PartitionSpec as P

F32 = jnp.float32
BF16 = jnp.bfloat16
MESH_ID = pl.DeviceIdType.MESH
NT = (((1,), (1,)), ((), ()))
NN = (((1,), (0,)), ((), ()))

GROUPS = 24
T_UNITS = 8
ROUNDS = 5
UNITS = T_UNITS + GROUPS * (GROUPS + 1) // 2
ROUND_GROUPS = ((23, 14), (13, 9), (8, 6), (5, 3), (2, 0))
COLORS = ((0, 88, (2, 1, 0)), (88, 88, (1, 0, 2)), (176, 80, (0, 2, 1)))
PLUS_PART = 1


def split3(a):
    a1 = a.astype(BF16)
    r1 = a - a1.astype(F32)
    a2 = r1.astype(BF16)
    a3 = (r1 - a2.astype(F32)).astype(BF16)
    return a1, a2, a3


def dot(a, b, dims):
    return lax.dot_general(a, b, dims, preferred_element_type=F32)


def dot6(a, b, dims):
    a1, a2, a3 = a
    b1, b2, b3 = b
    m = a1.shape[0]
    p1 = dot(jnp.concatenate([a1, a2, a3], axis=0), b1, dims)
    p2 = dot(jnp.concatenate([a1, a2], axis=0), b2, dims)
    p3 = dot(a1, b3, dims)
    low = p1[2 * m:] + p2[m:] + p3
    mid = p1[m:2 * m] + p2[:m]
    return p1[:m] + (mid + low)


def first_unit(k):
    return T_UNITS + (23 - k) * (24 - k) // 2


def kernel(vt_ref, tp_ref, zt_ref, out_ref, units, x_ref, v1_ref, v2_ref, v3_ref,
           acc_w, acc_g, acc_s, part, peer, a2a_send, a2a_recv, z_sem, ag_send, ag_recv, px_send, px_recv):
    row = lax.axis_index("row")
    col = lax.axis_index("col")
    coord = (col // 16, (col // 4) % 4, col % 4)
    oct_id = col // 8
    lane_row = pl.multiple_of(32 * (col % 8), 32)
    other = 1 - row

    def unit_at(i):
        return units.at[i // 64, (i // 16) % 4, (i // 4) % 4, i % 4]

    my_cols = pl.ds(pl.multiple_of(32 * row, 32), 32)
    z_keep = pltpu.make_async_copy(zt_ref.at[row], x_ref.at[:, my_cols, :], z_sem.at[0])
    z_send = pltpu.make_async_remote_copy(
        src_ref=zt_ref.at[other], dst_ref=x_ref.at[:, my_cols, :],
        send_sem=z_sem.at[1], recv_sem=z_sem.at[2],
        device_id={"row": other}, device_id_type=MESH_ID)
    z_keep.start()
    z_send.start()

    def place(src, i, sem):
        dst = unit_at(i).at[pl.ds(lane_row, 32), :]
        owner = i % 64

        @pl.when(owner == col)
        def _():
            pltpu.make_async_copy(src, dst, a2a_recv.at[i // 64]).start()

        @pl.when(owner != col)
        def _():
            pltpu.make_async_remote_copy(
                src_ref=src, dst_ref=dst, send_sem=sem, recv_sem=a2a_recv.at[i // 64],
                device_id={"col": owner}, device_id_type=MESH_ID).start()

    def place_done(src, i, sem):
        @pl.when(i % 64 != col)
        def _():
            pltpu.make_async_remote_copy(
                src_ref=src, dst_ref=unit_at(i).at[pl.ds(lane_row, 32), :],
                send_sem=sem, recv_sem=a2a_recv.at[i // 64],
                device_id={"col": i % 64}, device_id_type=MESH_ID).wait_send()

    def each_block(fn):
        fn(tp_ref, oct_id, a2a_send.at[3, 0])
        for t in (2, 1, 0):
            k = 8 * t + oct_id

            def one(b, carry):
                fn(vt_ref.at[t, b], first_unit(k) + b - k, a2a_send.at[t, b])
                return carry

            lax.fori_loop(k, GROUPS, one, 0)

    each_block(place)

    def wait_own_unit(r):
        def go():
            mine = unit_at(64 * r + col)
            pltpu.make_async_copy(mine, mine, a2a_recv.at[r]).wait()

        if 64 * (r + 1) <= UNITS:
            go()
        else:
            pl.when(64 * r + col < UNITS)(go)

    def block(r, c, free, fixed):
        lo, n, _ = COLORS[c]
        sel = []
        for ax in range(3):
            if ax in fixed:
                sel.append(fixed[ax])
            elif ax in free:
                sel.append(free[ax])
            else:
                sel.append(coord[ax])
        return units.at[(r, *sel, pl.ds(lo, n), slice(None))]

    def hop(r, c, n, ax, d, free, fixed):
        ref = block(r, c, free, fixed)
        tgt = [coord[0], coord[1], coord[2]]
        tgt[ax] = (coord[ax] + d) % 4
        return pltpu.make_async_remote_copy(
            src_ref=ref, dst_ref=ref, send_sem=ag_send.at[r, c, n], recv_sem=ag_recv.at[r, c, n],
            device_id={"col": 16 * tgt[0] + 4 * tgt[1] + tgt[2]}, device_id_type=MESH_ID)

    FULL = slice(None)

    def hops(r, c, phase, incoming):
        a1, a2, a3 = COLORS[c][2]
        if phase == 0:
            spec = [(0, a1, 1, {}, {}), (1, a1, 3, {}, {}), (2, a1, 2, {}, {})]
        elif phase == 1:
            spec = [(3 + i, a2, d, {a1: FULL}, {}) for i, d in enumerate((1, 3, 2))]
        elif phase == 2:
            spec = [(6 + i, a3, d, {a1: FULL, a2: FULL}, {}) for i, d in enumerate((1, 3))]
        else:
            o, f = min(a1, a2), max(a1, a2)
            spec = []
            for i, d, part_sl in ((8, 1, pl.ds(0, PLUS_PART)), (9, 3, pl.ds(PLUS_PART, 4 - PLUS_PART))):
                frm = (coord[a3] - d) % 4
                spec.append((i, a3, d, {o: part_sl, f: FULL}, {a3: frm}))
        out = []
        for n, ax, d, free, fixed in spec:
            if incoming:
                fixed = dict(fixed)
                fixed[ax] = (coord[ax] - d) % 4 if phase < 3 else (coord[ax] + 2) % 4
            out.append(hop(r, c, n, ax, d, free, fixed))
        return out

    def start(r, phase):
        for c in range(3):
            for h in hops(r, c, phase, False):
                h.start()

    def arrive(r, phase):
        for c in range(3):
            for h in hops(r, c, phase, True):
                h.wait_recv()

    ri = lax.broadcasted_iota(jnp.int32, (256, 256), 0) // 32
    ci = lax.broadcasted_iota(jnp.int32, (256, 256), 1) // 32

    def group(k, carry):
        base = first_unit(k)
        slot = k % 2
        acc_w[...] = jnp.zeros_like(acc_w)
        acc_g[...] = jnp.zeros_like(acc_g)
        acc_s[...] = jnp.zeros_like(acc_s)

        def inner(p, c2):
            i0 = base + jnp.maximum(2 * p, k) - k
            lo = unit_at(i0)[...]
            lo = jnp.where(2 * p >= k, lo, 0.0)
            hi = unit_at(base + 2 * p + 1 - k)[...]
            v1, v2, v3 = split3(jnp.concatenate([lo, hi], axis=1))
            v1_ref[p] = v1
            v2_ref[p] = v2
            v3_ref[p] = v3
            x1, x2, x3 = split3(x_ref[p])
            p1 = dot(jnp.concatenate([x1, x2, x3, v1, v2, v3], axis=0), v1, NT)
            p2 = dot(jnp.concatenate([x1, x2, v2], axis=0), v2, NT)
            p3 = dot(x1, v3, NT)
            acc_w[...] += p1[:64] + ((p1[64:128] + p2[:64]) + (p1[128:192] + p2[64:128] + p3))
            acc_g[...] += p1[192:448] + p2[128:384]
            acc_s[...] += p1[448:704] + p1[704:960]
            return c2

        lax.fori_loop(k // 2, 12, inner, 0)
        s = acc_s[...]
        part[slot, 0:64] = acc_w[...]
        part[slot, 64:320] = acc_g[...] + (s + s.T)
        swap = pltpu.make_async_remote_copy(
            src_ref=part.at[slot], dst_ref=peer.at[slot], send_sem=px_send.at[slot], recv_sem=px_recv.at[slot],
            device_id={"row": other}, device_id_type=MESH_ID)
        swap.start()
        swap.wait()
        wt = part[slot, 0:64] + peer[slot, 0:64]
        gram = part[slot, 64:320] + peer[slot, 64:320]

        tsel = unit_at(k % 8)[...]
        lane = lax.broadcasted_iota(jnp.int32, (256, 128), 1) // 32
        tm = jnp.where(lane == k // 8, tsel, 0.0)
        tm = tm + pltpu.roll(tm, 32, 1)
        tm = tm + pltpu.roll(tm, 64, 1)
        tf = jnp.where(ri == ci, jnp.concatenate([tm, tm], axis=1), 0.0)
        for lvl in (1, 2, 4):
            off = (ri // (2 * lvl) == ci // (2 * lvl)) & (ri // lvl < ci // lvl)
            ts = split3(tf)
            mid = dot6(split3(jnp.where(off, gram, 0.0)), ts, NN)
            tf = tf - dot6(ts, split3(mid), NN)
        y1, y2, y3 = split3(dot6(split3(wt), split3(tf), NT))
        y12 = jnp.concatenate([y1, y2], axis=0)
        y123 = jnp.concatenate([y1, y2, y3], axis=0)

        def update(p, c2):
            p1 = dot(y123, v1_ref[p], NN)
            p2 = dot(y12, v2_ref[p], NN)
            p3 = dot(y1, v3_ref[p], NN)
            x_ref[p] = x_ref[p] - (p1[:64] + ((p1[64:128] + p2[:64]) + (p1[128:192] + p2[64:128] + p3)))
            return c2

        lax.fori_loop(k // 2, 12, update, 0)
        return carry

    z_keep.wait()
    z_send.wait()
    for step in range(ROUNDS + 4):
        r = step - 3
        if 0 <= r < ROUNDS:
            arrive(r, 2)
            start(r, 3)
        r = step - 2
        if 0 <= r < ROUNDS:
            arrive(r, 1)
            start(r, 2)
        r = step - 1
        if 0 <= r < ROUNDS:
            arrive(r, 0)
            start(r, 1)
        if step < ROUNDS:
            wait_own_unit(step)
            start(step, 0)
        r = step - 4
        if 0 <= r < ROUNDS:
            arrive(r, 3)
            first, last = ROUND_GROUPS[r]
            lax.fori_loop(0, first - last + 1, lambda i, c, first=first: group(first - i, c), 0)

    keep = pltpu.make_async_copy(x_ref.at[:, my_cols, :], out_ref.at[row], z_sem.at[0])
    give = pltpu.make_async_remote_copy(
        src_ref=x_ref.at[:, pl.ds(pl.multiple_of(32 * other, 32), 32), :], dst_ref=out_ref.at[row],
        send_sem=z_sem.at[1], recv_sem=z_sem.at[2],
        device_id={"row": other}, device_id_type=MESH_ID)
    keep.start()
    give.start()
    each_block(place_done)
    for r in range(ROUNDS):
        for phase in range(4):
            for c in range(3):
                for h in hops(r, c, phase, False):
                    h.wait_send()
    keep.wait()
    give.wait()


def solution(mesh):
    def local_apply(v_loc, t_loc, z_loc):
        vt = v_loc.reshape(24, 128, 3, 32).transpose(2, 0, 3, 1)
        tp = jnp.concatenate([t_loc.transpose(1, 0, 2).reshape(32, 96), jnp.zeros((32, 32), F32)], axis=1)
        zt = z_loc.reshape(2, 12, 256, 32).transpose(0, 1, 3, 2)
        hbm = pl.BlockSpec(memory_space=pl.ANY)
        out = pl.pallas_call(
            kernel,
            out_shape=jax.ShapeDtypeStruct((2, 12, 32, 256), F32),
            in_specs=[hbm, hbm, hbm],
            out_specs=hbm,
            scratch_shapes=[
                pltpu.VMEM((ROUNDS, 4, 4, 4, 256, 128), F32),
                pltpu.VMEM((12, 64, 256), F32),
                pltpu.VMEM((12, 256, 256), BF16),
                pltpu.VMEM((12, 256, 256), BF16),
                pltpu.VMEM((12, 256, 256), BF16),
                pltpu.VMEM((64, 256), F32),
                pltpu.VMEM((256, 256), F32),
                pltpu.VMEM((256, 256), F32),
                pltpu.VMEM((2, 320, 256), F32),
                pltpu.VMEM((2, 320, 256), F32),
                pltpu.SemaphoreType.DMA((4, 24)),
                pltpu.SemaphoreType.DMA((ROUNDS,)),
                pltpu.SemaphoreType.DMA((3,)),
                pltpu.SemaphoreType.DMA((ROUNDS, 3, 10)),
                pltpu.SemaphoreType.DMA((ROUNDS, 3, 10)),
                pltpu.SemaphoreType.DMA((2,)),
                pltpu.SemaphoreType.DMA((2,)),
            ],
            compiler_params=pltpu.CompilerParams(has_side_effects=True, vmem_limit_bytes=67_000_000),
        )(vt, tp, zt)
        return out.transpose(0, 1, 3, 2).reshape(6144, 32)

    return jax.shard_map(
        local_apply,
        mesh=mesh,
        in_specs=(P("row", "col"), P("col", None, None), P(None, ("row", "col"))),
        out_specs=P(None, ("row", "col")),
        check_vma=False,
    )
```

time: 3380 us -> 341 us (0.10)
  matrix products: 1460 us -> 0 us
  blocking collectives: 1150 us -> 0 us
  waiting for transfers between devices: 720 us -> 0 us
  Pallas kernels: 0 us -> 331 us
    dot_general x576 -> x0, matrix products: 1460 us -> none  [the longest x192 765 us: inner_step(): lax.dot_general(v_blk, x_in, CONTRACT_ROWS, precision=FULL_PREC, preferre...]
    all_gather x3 -> x0, waiting for transfers between devices: 719 us -> none  [outer_step(): v_all = lax.all_gather(v_own, 'col')]
    psum x192 -> x0, blocking collectives: 664 us -> none  [inner_step(): w_sum = lax.psum(w_part, 'row')]
    all_gather x3 -> x0, blocking collectives: 487 us -> none  [outer_step(): t_all = lax.all_gather(t_own, 'col')]
    pallas_call x0 -> x1, Pallas kernels: none -> 331 us  [local_apply(): pl.pallas_call(kernel, out_shape=jax.ShapeDtypeStruct((2, 12, 32, 256), F...]
  transfers between devices with their start and end apart: 4 -> 0, of which waited for: 4 -> 0; matrix products, arithmetic and copies ran while one was open for 0% -> 0% of each run, Pallas kernels for 0% -> 0%
where the time goes in v1:
time: 341 us; the launch traced here: 339 us
  Pallas kernels  331 us (97%)
  local copies, waits for them, and re-layouts  7.62 us (2%)
    pallas_call x1, Pallas kernels, local_apply(): pl.pallas_call(kernel, out_shape=jax.ShapeDtypeStruct((2, 12, 32, 256), F...  331 us

profile of v1, /device:TPU:1, one launch (start us, length us, event | category | flops | bytes accessed | tf_op | source)
XLA Modules:
  0.0 338.8 jit_solution(6237668492977510355)
XLA Ops:
  0.0 1.5 copy.9
  1.5 0.0 copy-start
  1.5 1.2 copy.12
  2.7 0.0 copy-done
  2.7 0.2 reshape.14
  2.9 0.0 copy-start.1
  2.9 1.3 copy.13
  4.3 0.0 copy-done.1
  4.3 0.1 reshape.13
  4.4 0.6 concatenate.3.tp_ref
  5.0 331.1 %shard_map.37 = f32[2,12,32,256]{3,2,1,0:T(8,128)} custom-call(f32[3,24,32,128]{3,2,1,0:T(8,128)} %bitcast.18, f32[32,128]{1,0:T(8,128)} %concatenate.3.tp_ref, f32[2,12,32,256]{3,2,1,0:T(8,128)} %bitcast.19), custom_call_target="tpu_custom_call" | custom-call | tf_op jit(solution)/shard_map/pallas_call | solution.py:285
  336.1 1.6 copy.8
  337.8 1.0 reshape.15
  (1 shorter events, 0.0 us)
Async XLA Ops:
  1.5 1.2 copy-start
  2.9 1.4 copy-start.1
